TPU v7x, 32 devices: a whole 2x2x4 slice. The times are simulated.
32 devices in a mesh: ba: 8 (over y, x, core), wa: 4 (over z).
Axes of the slice: x: 2, y: 2, z: 4, core: 2. Of those that a mesh axis runs over, the one named last changes fastest.
Arguments:
- sky_model: float32 [2, 2048, 2048], P(None, None, 'wa'), may hold values from -6 to 6
- plane_w: float32 [8], P('ba'), may hold values from -60 to 60
- kernel: float32 [16, 8], replicated, may hold values from -2 to 2
- tile_ids: int32 [512], P(('ba', 'wa')), may hold values from 0 to 255, as said below
- plane_ids: int32 [512, 1], P(('ba', 'wa')), may hold values from 0 to 7; in each aligned block of 16 rows (0 to 15, 16 to 31, ...) at most 2 rows name the same one
- positions: int32 [512, 2, 512], P(('ba', 'wa')), may hold values from 0 to 1935
- observed: float32 [512, 2, 512], P(('ba', 'wa')), may hold values from -6 to 6
Outputs:
- residual_vis: float32 [512, 2, 512], P(('ba', 'wa'))
Inputs may be any that keep to these rules, and one draw needn't show every extreme that they name: `plane_ids`: among the 16 blocks of one device at most 2 name the same w-plane, and in every draw some device has a w-plane named by exactly 2 of its blocks. `tile_ids`: A tile id is row_tile * 16 + column_tile; the blocks held at index a of wa name column tiles a * 4 to (a + 1) * 4 - 1.
All inputs are finite; a program needn't handle non-finite values.
Results may differ from a plain program's by a relative error of at most 0.0003.
Values sent between devices are 32-bit elements; how exact they have to be, the bound alone decides.
A program may use at most 128 MiB of HBM per device.

v0:
```python
import math
import jax
import jax.numpy as jnp
from jax import lax
from jax.sharding import PartitionSpec as P

TILE = 128
PRECISE = lax.Precision.HIGHEST
FIELD_WIDTH = 0.7


def product(pattern, operand_a, operand_b):
    return jnp.einsum(pattern, operand_a, operand_b, precision=PRECISE)


def complex_product(pattern, table_pair, values):
    return (
        product(pattern, table_pair[0], values[0]) - product(pattern, table_pair[1], values[1]),
        product(pattern, table_pair[0], values[1]) + product(pattern, table_pair[1], values[0]),
    )


def phase_table(rows_count, cols_count, modulus):
    first_index = jnp.arange(rows_count, dtype=jnp.int32)[:, None]
    second_index = jnp.arange(cols_count, dtype=jnp.int32)[None, :]
    angle_rad = (first_index * second_index % modulus).astype(jnp.float32) * (
        -2.0 * math.pi / modulus
    )
    return (jnp.cos(angle_rad), jnp.sin(angle_rad))


def transform(values, pattern):
    length = values[0].shape[0]
    columns = values[0].shape[1]
    long_side = min(length, 128)
    short_side = length // long_side
    shaped = (
        values[0].reshape(long_side, short_side, columns),
        values[1].reshape(long_side, short_side, columns),
    )
    section_one = complex_product(
        "ab,anl->bnl", phase_table(long_side, long_side, long_side), shaped
    )
    twiddle = phase_table(long_side, short_side, length)
    twist_real = twiddle[0][:, :, None]
    twist_imag = twiddle[1][:, :, None]
    turned = (
        section_one[0] * twist_real - section_one[1] * twist_imag,
        section_one[0] * twist_imag + section_one[1] * twist_real,
    )
    return complex_product(
        "nk,bnl->" + pattern, phase_table(short_side, short_side, short_side), turned
    )


def kernel_rows(fine_position, kernel, tile_side):
    oversample, support = kernel.shape
    cell_index = fine_position // oversample
    offset_index = fine_position % oversample
    picker = (offset_index[..., None] == jnp.arange(oversample, dtype=jnp.int32)).astype(
        jnp.float32
    )
    kernel_taps = product("gso,ok->gsk", picker, kernel)
    tile_cells = jnp.arange(tile_side, dtype=jnp.int32)
    weights = jnp.zeros(fine_position.shape + (tile_side,), jnp.float32)
    for tap_step in range(support):
        weights = weights + jnp.where(
            tile_cells == cell_index[..., None] + tap_step,
            kernel_taps[..., tap_step : tap_step + 1],
            0.0,
        )
    return weights


def degrid(tiles, fine_position, kernel):
    tile_side = tiles.shape[-1]
    row_weights = kernel_rows(fine_position[:, 0], kernel, tile_side)
    col_weights = kernel_rows(fine_position[:, 1], kernel, tile_side)
    partial_value = product("gsu,gcuv->gcsv", row_weights, tiles)
    return jnp.sum(partial_value * col_weights[:, None], axis=-1)


def grouped(function, count, operands):
    group_size = math.gcd(count, 8)
    reshaped = tuple(
        (
            operand.reshape((count // group_size, group_size) + operand.shape[1:])
            for operand in operands
        )
    )

    def apply_group(group_items):
        return function(*group_items)

    result = lax.map(apply_group, reshaped)
    return result.reshape((count,) + result.shape[2:])


def shards(sky_model, plane_w, kernel, tile_ids, plane_ids, positions, observed):
    extent = sky_model.shape[1]
    column_count = sky_model.shape[2]
    slab_index = lax.axis_index("wa")
    spacing = FIELD_WIDTH / extent
    column_coord = (
        (slab_index * column_count + jnp.arange(column_count, dtype=jnp.int32)).astype(jnp.float32)
        - extent / 2
    ) * spacing
    row_coord = (jnp.arange(extent, dtype=jnp.int32).astype(jnp.float32) - extent / 2) * spacing
    radius_sq = row_coord[:, None] ** 2 + column_coord[None, :] ** 2
    lowered = -radius_sq / (1.0 + jnp.sqrt(1.0 - radius_sq))
    phase_angle = -2.0 * math.pi * plane_w[0] * lowered
    cosine = jnp.cos(phase_angle)
    sine_part = jnp.sin(phase_angle)
    image_real = sky_model[0] * cosine - sky_model[1] * sine_part
    image_imag = sky_model[0] * sine_part + sky_model[1] * cosine
    half_done = transform((image_real, image_imag), "lkb")
    stacked = jnp.stack(
        [half_done[0].reshape(column_count, extent), half_done[1].reshape(column_count, extent)]
    )
    exchanged = lax.all_to_all(stacked, "wa", split_axis=2, concat_axis=1, tiled=True)
    finished = transform((exchanged[0], exchanged[1]), "kbl")
    norm_factor = 1.0 / extent
    uv_grid = jnp.stack(
        [
            finished[0].reshape(extent, column_count) * norm_factor,
            finished[1].reshape(extent, column_count) * norm_factor,
        ]
    )
    plane_count = lax.axis_size("ba")
    block_count = tile_ids.shape[0]
    sample_count = positions.shape[2]
    capacity = max(2, block_count // plane_count)
    target = plane_ids[:, 0]
    onehot = (target[:, None] == jnp.arange(plane_count, dtype=jnp.int32)[None, :]).astype(
        jnp.int32
    )
    earlier = jnp.cumsum(onehot, axis=0) - onehot
    rank_in = jnp.sum(earlier * onehot, axis=1)
    slot_index = target * capacity + rank_in
    slot_tiles = jnp.zeros((plane_count * capacity,), jnp.int32).at[slot_index].set(tile_ids)
    slot_tiles = slot_tiles.reshape(plane_count, capacity)
    tile_side = TILE
    tiles_across = extent // tile_side
    local_across = column_count // tile_side

    def cut_tile(tile_number):
        row_tile = tile_number // tiles_across
        col_tile = tile_number % tiles_across - slab_index * local_across
        return lax.dynamic_slice(
            uv_grid,
            (jnp.int32(0), row_tile * tile_side, col_tile * tile_side),
            (2, tile_side, tile_side),
        )

    slot_fine = (
        jnp.zeros((plane_count * capacity, 2, sample_count), jnp.int32)
        .at[slot_index]
        .set(positions)
    )
    slot_fine = slot_fine.reshape(plane_count, capacity, 2, sample_count)
    asked_tiles = lax.all_to_all(slot_tiles, "ba", split_axis=0, concat_axis=0, tiled=True)
    asked_fine = lax.all_to_all(slot_fine, "ba", split_axis=0, concat_axis=0, tiled=True)
    count = asked_tiles.shape[0] * asked_tiles.shape[1]

    def slot_group(tile_group, fine_group):
        return degrid(jax.vmap(cut_tile)(tile_group), fine_group, kernel)

    values = grouped(
        slot_group, count, (asked_tiles.reshape(count), asked_fine.reshape(count, 2, sample_count))
    )
    values = values.reshape(asked_tiles.shape[0], asked_tiles.shape[1], 2, sample_count)
    answers = lax.all_to_all(values, "ba", split_axis=0, concat_axis=0, tiled=True)
    predicted = answers.reshape(plane_count * capacity, 2, sample_count)[slot_index]
    return observed - predicted


def solution(mesh):
    return jax.shard_map(
        shards,
        mesh=mesh,
        in_specs=(
            P(None, None, "wa"),
            P("ba"),
            P(),
            P(("ba", "wa")),
            P(("ba", "wa"), None),
            P(("ba", "wa"), None, None),
            P(("ba", "wa"), None, None),
        ),
        out_specs=P(("ba", "wa"), None, None),
        check_vma=False,
    )
```

profile of v0, /device:TPU:0, one launch (start us, length us, event | category | flops | bytes accessed | tf_op | source)
XLA Modules:
  0.0 576.1 jit_solution(2095315293875353910)
XLA Ops:
  3.7 5.2 all-to-all-start
  9.0 7.7 %fusion.226 = (f32[1,2048,512]{2,1,0:T(8,128)}, f32[1,2048,512]{2,1,0:T(8,128)}) fusion(f32[2,2048,512]{2,1,0:T(8,128)} %param.9), kind=kLoop, calls=%fused_computation.309 | loop fusion | bytes 16777216 | tf_op jit(solution)/shard_map/slice | solution.py:114
  17.3 34.6 %fusion.105 = f32[128,16,512]{2,0,1:T(8,128)S(1)} fusion(f32[128,16,512]{2,1,0:T(8,128)} %bitcast.269, f32[128,16,512]{2,1,0:T(8,128)} %bitcast.265, f32[512]{0:T(512)S(1)} %multiply_multiply_fusion.1, f32[128,16]{0,1:T(8,128)S(1)} %get-tuple-element.237, f32[]{:T(128)} %bitcast.16), kind=kOutput, calls=%fused_computation.193 | convolution fusion | flops 1620279296 | bytes 12593156 | tf_op jit(solution)/shard_map/ab,anl->bnl/dot_general | solution.py:13
  51.9 23.6 %fusion.103 = f32[128,16,512]{2,0,1:T(8,128)S(1)} fusion(f32[128,16,512]{2,1,0:T(8,128)S(1)} %bitcast.270, f32[128,16,512]{2,1,0:T(8,128)S(1)} %bitcast.266, f32[512]{0:T(512)S(1)} %multiply_multiply_fusion.1, f32[128,16]{0,1:T(8,128)S(1)} %get-tuple-element.237, f32[]{:T(128)} %bitcast.16), kind=kOutput, calls=%fused_computation.191 | convolution fusion | flops 1620279296 | bytes 12593156 | tf_op jit(solution)/shard_map/ab,anl->bnl/dot_general | solution.py:13
  75.6 24.7 %convolution_subtract_fusion = f32[128,16,512]{2,0,1:T(8,128)} fusion(f32[128,16,512]{2,0,1:T(8,128)S(1)} %fusion.105, f32[128,16,512]{2,1,0:T(8,128)S(1)} %bitcast.271, f32[128,16,512]{2,1,0:T(8,128)S(1)} %bitcast.267, f32[512]{0:T(512)S(1)} %multiply_multiply_fusion.1, f32[128,16]{0,1:T(8,128)S(1)} %get-tuple-element.237, f32[]{:T(128)} %bitcast.16), kind=kOutput, calls=%fused_computation.176 | convolution fusion | flops 1621327872 | bytes 16787460 | tf_op jit(solution)/shard_map/ab,anl->bnl/dot_general | solution.py:13
  100.3 25.9 %multiply_subtract_fusion.1 = (f32[128,16,512]{2,0,1:T(8,128)S(1)}, f32[128,16,512]{2,0,1:T(8,128)S(1)}) fusion(f32[128,16,512]{2,0,1:T(8,128)} %convolution_subtract_fusion, f32[128,16]{0,1:T(8,128)S(1)} %get-tuple-element.238, f32[128,16]{0,1:T(8,128)S(1)} %fusion.142, f32[128,16,512]{2,0,1:T(8,128)S(1)} %fusion.103, f32[128,16,512]{2,1,0:T(8,128)S(1)} %bitcast.272, ...), kind=kOutput, calls=%fused_computation.146 | convolution fusion | flops 1627619328 | bytes 25192452 | tf_op jit(solution)/shard_map/ab,anl->bnl/dot_general | solution.py:13
  126.3 6.6 %fusion.72 = f32[128,512,16]{1,2,0:T(8,128)S(1)} fusion(f32[128,16,512]{2,0,1:T(8,128)S(1)} %get-tuple-element.232), kind=kOutput, calls=%fused_computation.167 | convolution fusion | flops 201330176 | bytes 8388608 | tf_op jit(solution)/shard_map/nk,bnl->lkb/dot_general | solution.py:13
  132.8 6.8 %fusion.70 = f32[128,512,16]{1,2,0:T(8,128)S(1)} fusion(f32[128,16,512]{2,0,1:T(8,128)S(1)} %get-tuple-element.232), kind=kOutput, calls=%fused_computation.165 | convolution fusion | flops 201330176 | bytes 8388608 | tf_op jit(solution)/shard_map/nk,bnl->lkb/dot_general | solution.py:13
  139.7 7.1 %subtract_bitcast_fusion = f32[512,16,128]{0,1,2:T(8,128)S(1)} fusion(f32[128,512,16]{1,2,0:T(8,128)S(1)} %fusion.72, f32[128,16,512]{2,0,1:T(8,128)S(1)} %get-tuple-element.231), kind=kOutput, calls=%fused_computation.144 | convolution fusion | flops 202378752 | bytes 12582912 | tf_op jit(solution)/shard_map/nk,bnl->lkb/dot_general | solution.py:13
  149.2 7.4 %add_bitcast_fusion = f32[512,16,128]{0,1,2:T(8,128)S(1)} fusion(f32[128,512,16]{1,2,0:T(8,128)S(1)} %fusion.70, f32[128,16,512]{2,0,1:T(8,128)S(1)} %get-tuple-element.231), kind=kOutput, calls=%fused_computation.143 | convolution fusion | flops 202378752 | bytes 12582912 | tf_op jit(solution)/shard_map/nk,bnl->lkb/dot_general | solution.py:13
  160.0 16.5 %copy.84 = f32[2,512,2048]{1,0,2:T(2,128)} copy(f32[2,512,2048]{1,2,0:T(8,128)S(1)} %pad_maximum_fusion) | data formatting | bytes 16777216 | tf_op jit(solution)/shard_map/stack | solution.py:117
  176.5 5.8 %all-to-all-start.1 = ((f32[2,512,2048]{1,0,2:T(2,128)}), f32[2,512,2048]{1,0,2:T(2,128)}, u32[]{:S(2)}, u32[]{:S(2)}) async-start(f32[2,512,2048]{1,0,2:T(2,128)} %copy.84), calls=%async_computation.1 | async-start | bytes 16777216 | tf_op jit(solution)/shard_map/all_to_all | solution.py:120
  186.3 180.0 %all-to-all-done.1 = f32[2,512,2048]{1,0,2:T(2,128)} async-done(((f32[2,512,2048]{1,0,2:T(2,128)}), f32[2,512,2048]{1,0,2:T(2,128)}, u32[]{:S(2)}, u32[]{:S(2)}) %all-to-all-start.1) | async-done | bytes 8388640 | tf_op jit(solution)/shard_map/all_to_all | solution.py:120
  370.3 5.0 copy.85
  379.6 5.3 copy.88
  384.9 10.2 %fusion.64 = f32[128,16,512]{2,0,1:T(8,128)} fusion(f32[128,16,512]{2,1,0:T(8,128)} %bitcast.256), kind=kOutput, calls=%fused_computation.159 | convolution fusion | flops 1610842112 | bytes 8388608 | tf_op jit(solution)/shard_map/ab,anl->bnl/dot_general | solution.py:13
  395.1 7.1 %fusion.62 = f32[128,16,512]{2,0,1:T(8,128)} fusion(f32[128,16,512]{2,1,0:T(8,128)S(1)} %bitcast.257), kind=kOutput, calls=%fused_computation.157 | convolution fusion | flops 1610842112 | bytes 8388608 | tf_op jit(solution)/shard_map/ab,anl->bnl/dot_general | solution.py:13
  402.3 5.6 copy.86
  407.9 9.9 %fusion.82 = f32[128,16,512]{2,0,1:T(8,128)S(1)} fusion(f32[128,16,512]{2,0,1:T(8,128)} %fusion.64, f32[128,16,512]{2,1,0:T(8,128)} %bitcast.254), kind=kOutput, calls=%fused_computation.173 | convolution fusion | flops 1611890688 | bytes 12582912 | tf_op jit(solution)/shard_map/ab,anl->bnl/dot_general | solution.py:13
  417.8 7.5 %multiply_subtract_fusion = (f32[128,16,512]{2,0,1:T(8,128)S(1)}, f32[128,16,512]{2,0,1:T(8,128)S(1)}) fusion(f32[128,16,512]{2,0,1:T(8,128)S(1)} %fusion.82, f32[128,16]{0,1:T(8,128)S(1)} %get-tuple-element.238, f32[128,16]{0,1:T(8,128)S(1)} %fusion.142, f32[128,16,512]{2,0,1:T(8,128)S(1)} %copy-done.2, f32[128,16,512]{2,1,0:T(8,128)S(1)} %bitcast.255), kind=kOutput, calls=%fused_computation.142 | convolution fusion | flops 1618182144 | bytes 20987904 | tf_op jit(solution)/shard_map/ab,anl->bnl/dot_general | solution.py:13
  425.3 5.6 fusion.56
  430.9 5.8 %fusion.54 = f32[16,128,512]{2,0,1:T(8,128)S(1)} fusion(f32[128,16,512]{2,0,1:T(8,128)S(1)} %get-tuple-element.230), kind=kOutput, calls=%fused_computation.149 | convolution fusion | flops 201330176 | bytes 8388608 | tf_op jit(solution)/shard_map/nk,bnl->kbl/dot_general | solution.py:13
  436.7 6.1 %subtract_multiply_fusion = f32[16,128,512]{2,0,1:T(8,128)S(1)} fusion(f32[16,128,512]{2,0,1:T(8,128)S(1)} %fusion.56, f32[128,16,512]{2,0,1:T(8,128)S(1)} %get-tuple-element.229), kind=kOutput, calls=%fused_computation.140 | convolution fusion | flops 203427328 | bytes 12582912 | tf_op jit(solution)/shard_map/nk,bnl->kbl/dot_general | solution.py:13
  445.2 6.0 %add_multiply_fusion = f32[16,128,512]{2,0,1:T(8,128)S(1)} fusion(f32[16,128,512]{2,0,1:T(8,128)S(1)} %fusion.54, f32[128,16,512]{2,0,1:T(8,128)S(1)} %get-tuple-element.229), kind=kOutput, calls=%fused_computation.139 | convolution fusion | flops 203427328 | bytes 12582912 | tf_op jit(solution)/shard_map/nk,bnl->kbl/dot_general | solution.py:13
  457.9 107.1 %while.16 = (s32[]{:T(128)}, f32[2,8,2,512]{3,2,1,0:T(2,128)}, s32[2,8]{1,0:T(2,128)S(1)}, s32[]{:T(128)}, f32[2,2048,512]{2,1,0:T(8,128)}, /*index=5*/s32[2,8,2...) while((s32[]{:T(128)}, f32[2,8,2,512]{3,2,1,0:T(2,128)}, ...), condition=%wide.region_6.7_spmd, body=%wide.region_4.6_spmd.sunk | while | flops 1649795328 | bytes 12208282 | solution.py:95
  458.4 8.9 %select_add_fusion.2 = f32[8,512,128]{2,1,0:T(8,128)S(1)} fusion(f32[8,512]{1,0:T(8,128)S(1)} %bitcast.273, s32[8,512]{1,0:T(8,128)S(1)} %get-tuple-element.360, f32[8,512]{1,0:T(8,128)S(1)} %bitcast.274, s32[8,512]{1,0:T(8,128)S(1)} %get-tuple-element.362, f32[8,512]{1,0:T(8,128)S(1)} %bitcast.275, s32[8,512]{1,0:T(8,128)S(1)} %get-tuple-element.364, ...), kind=kLoop, calls=%fused_computation.8.clone.1 | loop fusion | flops 12058624 | bytes 2359296 | tf_op jit(solution)/shard_map/while/body/eval_jaxpr/add | solution.py:67
  469.7 23.6 %while.17 = (s32[]{:T(128)}, f32[2,2048,512]{2,1,0:T(8,128)}, s32[8,3]{0,1:T(4,128)S(1)}, f32[8,2,128,128]{3,2,1,0:T(8,128)S(1)}, s32[]{:T(128)}) while((s32[]{:T(128)}, f32[2,2048,512]{2,1,0:T(8,128)}, s32[8,3]{0,1:T(4,128)S(1)}, f32[8,2,128,128]{3,2,1,0:T(8,128)S(1)}, s32[]{:T(128)}) %tuple.108), condition=%wide.while_cond, body=%wide.while_body.sunk | while | flops 2 | bytes 262261 | solution.py:149
  493.3 17.5 %fusion.249 = f32[8,2,512]{2,1,0:T(2,128)S(1)} fusion(f32[8,2,128,128]{3,2,1,0:T(8,128)S(1)} %get-tuple-element.354, f32[8,512,128]{1,2,0:T(8,128)} %copy.239, f32[8,512]{1,0:T(8,128)S(1)} %bitcast.282, s32[8,512]{1,0:T(8,128)S(1)} %get-tuple-element.377, f32[8,512]{1,0:T(8,128)S(1)} %bitcast.283, s32[8,512]{1,0:T(8,128)S(1)} %get-tuple-element.379, ...), kind=kOutput, calls=%fused_computation.6.clone.2 | convolution fusion | flops 1624760320 | bytes 3440640 | tf_op jit(solution)/shard_map/while/body/eval_jaxpr/gsu,gcuv->gcsv/dot_general | solution.py:13
  511.9 8.9 %select_add_fusion.2 = f32[8,512,128]{2,1,0:T(8,128)S(1)} fusion(f32[8,512]{1,0:T(8,128)S(1)} %bitcast.273, s32[8,512]{1,0:T(8,128)S(1)} %get-tuple-element.360, f32[8,512]{1,0:T(8,128)S(1)} %bitcast.274, s32[8,512]{1,0:T(8,128)S(1)} %get-tuple-element.362, f32[8,512]{1,0:T(8,128)S(1)} %bitcast.275, s32[8,512]{1,0:T(8,128)S(1)} %get-tuple-element.364, ...), kind=kLoop, calls=%fused_computation.8.clone.1 | loop fusion | flops 12058624 | bytes 2359296 | tf_op jit(solution)/shard_map/while/body/eval_jaxpr/add | solution.py:67
  523.3 23.7 %while.17 = (s32[]{:T(128)}, f32[2,2048,512]{2,1,0:T(8,128)}, s32[8,3]{0,1:T(4,128)S(1)}, f32[8,2,128,128]{3,2,1,0:T(8,128)S(1)}, s32[]{:T(128)}) while((s32[]{:T(128)}, f32[2,2048,512]{2,1,0:T(8,128)}, s32[8,3]{0,1:T(4,128)S(1)}, f32[8,2,128,128]{3,2,1,0:T(8,128)S(1)}, s32[]{:T(128)}) %tuple.108), condition=%wide.while_cond, body=%wide.while_body.sunk | while | flops 2 | bytes 262261 | solution.py:149
  546.9 17.5 %fusion.249 = f32[8,2,512]{2,1,0:T(2,128)S(1)} fusion(f32[8,2,128,128]{3,2,1,0:T(8,128)S(1)} %get-tuple-element.354, f32[8,512,128]{1,2,0:T(8,128)} %copy.239, f32[8,512]{1,0:T(8,128)S(1)} %bitcast.282, s32[8,512]{1,0:T(8,128)S(1)} %get-tuple-element.377, f32[8,512]{1,0:T(8,128)S(1)} %bitcast.283, s32[8,512]{1,0:T(8,128)S(1)} %get-tuple-element.379, ...), kind=kOutput, calls=%fused_computation.6.clone.2 | convolution fusion | flops 1624760320 | bytes 3440640 | tf_op jit(solution)/shard_map/while/body/eval_jaxpr/gsu,gcuv->gcsv/dot_general | solution.py:13
  569.4 5.0 all-to-all-done.3
  (157 shorter events, 90.2 us)
Async XLA Ops:
  3.7 172.8 %all-to-all-start = ((s32[8,1,2]{2,1,0:T(1,128)}), s32[8,1,2]{2,1,0:T(1,128)S(1)}, u32[]{:S(2)}, u32[]{:S(2)}) async-start(s32[8,1,2]{2,1,0:T(1,128)} %bitcast.12), calls=%async_computation | async-start | bytes 8192 | tf_op jit(solution)/shard_map/all_to_all | solution.py:161
  17.3 34.6 %copy-start.3 = (f32[1,2048,512]{2,1,0:T(8,128)S(1)}, f32[1,2048,512]{2,1,0:T(8,128)}, u32[]{:S(2)}) copy-start(f32[1,2048,512]{2,1,0:T(8,128)} %get-tuple-element.235) | copy-start | bytes 12582916
  17.3 34.6 %copy-start.4 = (f32[1,2048,512]{2,1,0:T(8,128)S(1)}, f32[1,2048,512]{2,1,0:T(8,128)}, u32[]{:S(2)}) copy-start(f32[1,2048,512]{2,1,0:T(8,128)} %get-tuple-element.236) | copy-start | bytes 12582916
  176.5 6.4 %copy-start.6 = (s32[16,2,512]{2,1,0:T(2,128)S(1)}, s32[16,2,512]{2,1,0:T(2,128)}, u32[]{:S(2)}) copy-start(s32[16,2,512]{2,1,0:T(2,128)} %param.14) | copy-start | bytes 196612
  176.5 189.8 %all-to-all-start.1 = ((f32[2,512,2048]{1,0,2:T(2,128)}), f32[2,512,2048]{1,0,2:T(2,128)}, u32[]{:S(2)}, u32[]{:S(2)}) async-start(f32[2,512,2048]{1,0,2:T(2,128)} %copy.84), calls=%async_computation.1 | async-start | bytes 16777216 | tf_op jit(solution)/shard_map/all_to_all | solution.py:120
  366.3 91.6 %all-to-all-start.2 = ((s32[8,2,2,512]{3,2,1,0:T(2,128)}), s32[8,2,2,512]{3,2,1,0:T(2,128)S(1)}, u32[]{:S(2)}, u32[]{:S(2)}) async-start(s32[8,2,2,512]{3,2,1,0:T(2,128)} %bitcast.31), calls=%async_computation.2 | async-start | bytes 131072 | tf_op jit(solution)/shard_map/all_to_all | solution.py:162
  384.9 10.2 %copy-start.1 = (f32[1,4,512,512]{3,2,1,0:T(8,128)S(1)}, f32[1,4,512,512]{3,2,1,0:T(8,128)}, u32[]{:S(2)}) copy-start(f32[1,4,512,512]{3,2,1,0:T(8,128)} %copy.88) | copy-start | bytes 12582916
  407.9 9.9 %copy-start = (f32[1,4,512,512]{3,2,1,0:T(8,128)S(1)}, f32[1,4,512,512]{3,2,1,0:T(8,128)}, u32[]{:S(2)}) copy-start(f32[1,4,512,512]{3,2,1,0:T(8,128)} %copy.86) | copy-start | bytes 12582916
  407.9 9.9 %copy-start.2 = (f32[128,16,512]{2,0,1:T(8,128)S(1)}, f32[128,16,512]{2,0,1:T(8,128)}, u32[]{:S(2)}) copy-start(f32[128,16,512]{2,0,1:T(8,128)} %fusion.62) | copy-start | bytes 12582916
  453.7 4.2 copy-start.5
  457.9 117.1 %copy-start.7 = (f32[16,2,512]{2,1,0:T(2,128)S(1)}, f32[16,2,512]{2,1,0:T(2,128)}, u32[]{:S(2)}) copy-start(f32[16,2,512]{2,1,0:T(2,128)} %param.15) | copy-start | bytes 196612
  565.0 9.4 %all-to-all-start.3 = ((f32[8,2,2,512]{3,2,1,0:T(2,128)}), f32[8,2,2,512]{3,2,1,0:T(2,128)S(1)}, u32[]{:S(2)}, u32[]{:S(2)}) async-start(f32[8,2,2,512]{3,2,1,0:T(2,128)} %bitcast.33), calls=%async_computation.3 | async-start | bytes 131072 | tf_op jit(solution)/shard_map/all_to_all | solution.py:172
where the time goes:
time: 587 us; the launch traced here: 576 us
  matrix products  231 us (39%)
  waiting for transfers between devices  185 us (32%)
  local copies, waits for them, and re-layouts  112 us (19%)
  other arithmetic  27.1 us (5%)
  starting transfers between devices  19.3 us (3%)
    dot_general x22, matrix products, product(): return jnp.einsum(pattern, operand_a, operand_b, precision=PRECISE)  231 us
    all_to_all x1, waiting for transfers between devices, shards(): lax.all_to_all(stacked, 'wa', split_axis=2, concat_axis=1, tiled=True)  180 us
    gather x48, local copies, waits for them, and re-layouts  47 us
    add x2, other arithmetic, kernel_rows(): weights + jnp.where(tile_cells == cell_index[..., None] + tap_step, kerne...  17.9 us
    another operation x1, local copies, waits for them, and re-layouts, shards(): jnp.stack([half_done[0].reshape(column_count, extent), half_done[1].resha...  16.5 us
    slice x3, local copies, waits for them, and re-layouts, shards(): finished = transform((exchanged[0], exchanged[1]), 'kbl')  15.2 us
  transfers between devices with their start and end apart: 4, of which 2 were waited for; matrix products, arithmetic and copies ran while one was open for 45% of the time, Pallas kernels for 0%

commit v1 on v0

--- a/solution.py
+++ b/solution.py
@@ -117,7 +117,10 @@
     stacked = jnp.stack(
         [half_done[0].reshape(column_count, extent), half_done[1].reshape(column_count, extent)]
     )
-    exchanged = lax.all_to_all(stacked, "wa", split_axis=2, concat_axis=1, tiled=True)
+    exchanged = jnp.concatenate(
+        lax.all_to_all(jnp.stack(jnp.split(stacked, lax.axis_size("wa"), axis=2)), "wa", 0, 0),
+        axis=1,
+    )
     finished = transform((exchanged[0], exchanged[1]), "kbl")
     norm_factor = 1.0 / extent
     uv_grid = jnp.stack(

time: 587 us -> 566 us (0.964)
  local copies, waits for them, and re-layouts: 112 us -> 95.1 us
  matrix products: 231 us -> 222 us
    another operation x3 -> x2, local copies, waits for them, and re-layouts: 16.5 us -> 0.01 us  [the longest x1 16.5 us: shards(): jnp.stack([half_done[0].reshape(column_count, extent), half_done[1].resha...]
    dot_general x22, matrix products: 231 us -> 222 us  [product(): return jnp.einsum(pattern, operand_a, operand_b, precision=PRECISE)]
  transfers between devices with their start and end apart: 4 -> 4, of which waited for: 2 -> 2; matrix products, arithmetic and copies ran while one was open for 45% -> 42% of each run, Pallas kernels for 0% -> 0%
where the time goes in v1:
time: 566 us; the launch traced here: 555 us
  matrix products  222 us (39%)
  waiting for transfers between devices  185 us (33%)
  local copies, waits for them, and re-layouts  95.1 us (17%)
  other arithmetic  31 us (5%)
  starting transfers between devices  19.3 us (3%)
    dot_general x22, matrix products, product(): return jnp.einsum(pattern, operand_a, operand_b, precision=PRECISE)  222 us
    all_to_all x1, waiting for transfers between devices, shards(): lax.all_to_all(jnp.stack(jnp.split(stacked, lax.axis_size('wa'), axis=2))...  180 us
    gather x48, local copies, waits for them, and re-layouts  48.4 us
    slice x3, local copies, waits for them, and re-layouts, shards(): finished = transform((exchanged[0], exchanged[1]), 'kbl')  18.4 us
    add x2, other arithmetic, kernel_rows(): weights + jnp.where(tile_cells == cell_index[..., None] + tap_step, kerne...  17.9 us
  transfers between devices with their start and end apart: 4, of which 2 were waited for; matrix products, arithmetic and copies ran while one was open for 42% of the time, Pallas kernels for 0%

profile of v1, /device:TPU:0, one launch (start us, length us, event | category | flops | bytes accessed | tf_op | source)
XLA Modules:
  0.0 554.7 jit_solution(4152562422710093425)
XLA Ops:
  3.7 5.2 all-to-all-start
  9.0 7.7 %fusion.233 = (f32[1,2048,512]{2,1,0:T(8,128)}, f32[1,2048,512]{2,1,0:T(8,128)}) fusion(f32[2,2048,512]{2,1,0:T(8,128)} %param.9), kind=kLoop, calls=%fused_computation.323 | loop fusion | bytes 16777216 | tf_op jit(solution)/shard_map/slice | solution.py:114
  17.3 26.0 %fusion.112 = f32[128,16,512]{2,0,1:T(8,128)S(1)} fusion(f32[128,16,512]{2,1,0:T(8,128)} %bitcast.274, f32[128,16,512]{2,1,0:T(8,128)} %bitcast.270, f32[512]{0:T(512)S(1)} %multiply_multiply_fusion.1, f32[128,16]{0,1:T(8,128)S(1)} %get-tuple-element.234, f32[]{:T(128)} %bitcast.16), kind=kOutput, calls=%fused_computation.207 | convolution fusion | flops 1620279296 | bytes 12593156 | tf_op jit(solution)/shard_map/ab,anl->bnl/dot_general | solution.py:13
  43.4 23.4 %fusion.110 = f32[128,16,512]{2,0,1:T(8,128)S(1)} fusion(f32[128,16,512]{2,1,0:T(8,128)S(1)} %bitcast.275, f32[128,16,512]{2,1,0:T(8,128)S(1)} %bitcast.271, f32[512]{0:T(512)S(1)} %multiply_multiply_fusion.1, f32[128,16]{0,1:T(8,128)S(1)} %get-tuple-element.234, f32[]{:T(128)} %bitcast.16), kind=kOutput, calls=%fused_computation.205 | convolution fusion | flops 1620279296 | bytes 12593156 | tf_op jit(solution)/shard_map/ab,anl->bnl/dot_general | solution.py:13
  66.9 24.7 %convolution_subtract_fusion = f32[128,16,512]{2,0,1:T(8,128)} fusion(f32[128,16,512]{2,0,1:T(8,128)S(1)} %fusion.112, f32[128,16,512]{2,1,0:T(8,128)S(1)} %bitcast.276, f32[128,16,512]{2,1,0:T(8,128)S(1)} %bitcast.272, f32[512]{0:T(512)S(1)} %multiply_multiply_fusion.1, f32[128,16]{0,1:T(8,128)S(1)} %get-tuple-element.234, f32[]{:T(128)} %bitcast.16), kind=kOutput, calls=%fused_computation.182 | convolution fusion | flops 1621327872 | bytes 16787460 | tf_op jit(solution)/shard_map/ab,anl->bnl/dot_general | solution.py:13
  91.6 25.9 %multiply_subtract_fusion.1 = (f32[128,16,512]{2,0,1:T(8,128)S(1)}, f32[128,16,512]{2,0,1:T(8,128)S(1)}) fusion(f32[128,16,512]{2,0,1:T(8,128)} %convolution_subtract_fusion, f32[128,16]{0,1:T(8,128)S(1)} %get-tuple-element.235, f32[128,16]{0,1:T(8,128)S(1)} %fusion.149, f32[128,16,512]{2,0,1:T(8,128)S(1)} %fusion.110, f32[128,16,512]{2,1,0:T(8,128)S(1)} %bitcast.277, ...), kind=kOutput, calls=%fused_computation.152 | convolution fusion | flops 1627619328 | bytes 25192452 | tf_op jit(solution)/shard_map/ab,anl->bnl/dot_general | solution.py:13
  117.5 6.6 %fusion.70 = f32[128,512,16]{1,2,0:T(8,128)S(1)} fusion(f32[128,16,512]{2,0,1:T(8,128)S(1)} %get-tuple-element.225), kind=kOutput, calls=%fused_computation.171 | convolution fusion | flops 201330176 | bytes 8388608 | tf_op jit(solution)/shard_map/nk,bnl->lkb/dot_general | solution.py:13
  124.1 6.8 %fusion.72 = f32[128,512,16]{1,2,0:T(8,128)S(1)} fusion(f32[128,16,512]{2,0,1:T(8,128)S(1)} %get-tuple-element.225), kind=kOutput, calls=%fused_computation.173 | convolution fusion | flops 201330176 | bytes 8388608 | tf_op jit(solution)/shard_map/nk,bnl->lkb/dot_general | solution.py:13
  130.9 7.0 %add_bitcast_fusion = f32[512,16,128]{0,1,2:T(8,128)S(1)} fusion(f32[128,512,16]{1,2,0:T(8,128)S(1)} %fusion.70, f32[128,16,512]{2,0,1:T(8,128)S(1)} %get-tuple-element.224), kind=kOutput, calls=%fused_computation.149 | convolution fusion | flops 202378752 | bytes 12582912 | tf_op jit(solution)/shard_map/nk,bnl->lkb/dot_general | solution.py:13
  140.4 7.5 %subtract_bitcast_fusion = f32[512,16,128]{0,1,2:T(8,128)S(1)} fusion(f32[128,512,16]{1,2,0:T(8,128)S(1)} %fusion.72, f32[128,16,512]{2,0,1:T(8,128)S(1)} %get-tuple-element.224), kind=kOutput, calls=%fused_computation.150 | convolution fusion | flops 202378752 | bytes 12582912 | tf_op jit(solution)/shard_map/nk,bnl->lkb/dot_general | solution.py:13
  155.3 5.8 %all-to-all-start.1 = ((f32[4,2,512,512]{2,3,1,0:T(8,128)}), f32[4,2,512,512]{2,3,1,0:T(8,128)}, u32[]{:S(2)}, u32[]{:S(2)}) async-start(f32[4,2,512,512]{2,3,1,0:T(8,128)} %pad_maximum_fusion), calls=%async_computation.1 | async-start | bytes 16777216 | tf_op jit(solution)/shard_map/all_to_all | solution.py:121
  165.1 180.1 %all-to-all-done.1 = f32[4,2,512,512]{2,3,1,0:T(8,128)} async-done(((f32[4,2,512,512]{2,3,1,0:T(8,128)}), f32[4,2,512,512]{2,3,1,0:T(8,128)}, u32[]{:S(2)}, u32[]{:S(2)}) %all-to-all-start.1) | async-done | bytes 8388640 | tf_op jit(solution)/shard_map/all_to_all | solution.py:121
  349.1 7.7 %fusion.232 = (f32[1,4,512,512]{2,3,0,1:T(8,128)}, f32[1,4,512,512]{2,3,0,1:T(8,128)}) fusion(f32[2,4,512,512]{2,3,0,1:T(8,128)} %bitcast.28), kind=kLoop, calls=%fused_computation.322 | loop fusion | bytes 16777216 | tf_op jit(solution)/shard_map/slice | solution.py:124
  356.8 5.3 copy.62
  362.1 10.2 %fusion.64 = f32[128,16,512]{2,0,1:T(8,128)} fusion(f32[128,16,512]{2,1,0:T(8,128)} %bitcast.262), kind=kOutput, calls=%fused_computation.165 | convolution fusion | flops 1610842112 | bytes 8388608 | tf_op jit(solution)/shard_map/ab,anl->bnl/dot_general | solution.py:13
  372.3 7.2 %fusion.62 = f32[128,16,512]{2,0,1:T(8,128)} fusion(f32[128,16,512]{2,1,0:T(8,128)S(1)} %bitcast.263), kind=kOutput, calls=%fused_computation.163 | convolution fusion | flops 1610842112 | bytes 8388608 | tf_op jit(solution)/shard_map/ab,anl->bnl/dot_general | solution.py:13
  379.5 5.4 copy.60
  385.0 9.9 %fusion.82 = f32[128,16,512]{2,0,1:T(8,128)S(1)} fusion(f32[128,16,512]{2,0,1:T(8,128)} %fusion.64, f32[128,16,512]{2,1,0:T(8,128)} %bitcast.260), kind=kOutput, calls=%fused_computation.179 | convolution fusion | flops 1611890688 | bytes 12582912 | tf_op jit(solution)/shard_map/ab,anl->bnl/dot_general | solution.py:13
  394.9 7.7 %multiply_subtract_fusion = (f32[128,16,512]{2,0,1:T(8,128)S(1)}, f32[128,16,512]{2,0,1:T(8,128)S(1)}) fusion(f32[128,16,512]{2,0,1:T(8,128)S(1)} %fusion.82, f32[128,16]{0,1:T(8,128)S(1)} %get-tuple-element.235, f32[128,16]{0,1:T(8,128)S(1)} %fusion.149, f32[128,16,512]{2,0,1:T(8,128)S(1)} %copy-done.2, f32[128,16,512]{2,1,0:T(8,128)S(1)} %bitcast.261), kind=kOutput, calls=%fused_computation.148 | convolution fusion | flops 1618182144 | bytes 20987904 | tf_op jit(solution)/shard_map/ab,anl->bnl/dot_general | solution.py:13
  402.6 5.6 %fusion.56 = f32[16,128,512]{2,0,1:T(8,128)S(1)} fusion(f32[128,16,512]{2,0,1:T(8,128)S(1)} %get-tuple-element.223), kind=kOutput, calls=%fused_computation.157 | convolution fusion | flops 201330176 | bytes 8388608 | tf_op jit(solution)/shard_map/nk,bnl->kbl/dot_general | solution.py:13
  408.2 5.8 %fusion.54 = f32[16,128,512]{2,0,1:T(8,128)S(1)} fusion(f32[128,16,512]{2,0,1:T(8,128)S(1)} %get-tuple-element.223), kind=kOutput, calls=%fused_computation.155 | convolution fusion | flops 201330176 | bytes 8388608 | tf_op jit(solution)/shard_map/nk,bnl->kbl/dot_general | solution.py:13
  414.0 6.1 %subtract_multiply_fusion = f32[16,128,512]{2,0,1:T(8,128)S(1)} fusion(f32[16,128,512]{2,0,1:T(8,128)S(1)} %fusion.56, f32[128,16,512]{2,0,1:T(8,128)S(1)} %get-tuple-element.222), kind=kOutput, calls=%fused_computation.146 | convolution fusion | flops 203427328 | bytes 12582912 | tf_op jit(solution)/shard_map/nk,bnl->kbl/dot_general | solution.py:13
  422.5 6.0 %add_multiply_fusion = f32[16,128,512]{2,0,1:T(8,128)S(1)} fusion(f32[16,128,512]{2,0,1:T(8,128)S(1)} %fusion.54, f32[128,16,512]{2,0,1:T(8,128)S(1)} %get-tuple-element.222), kind=kOutput, calls=%fused_computation.145 | convolution fusion | flops 203427328 | bytes 12582912 | tf_op jit(solution)/shard_map/nk,bnl->kbl/dot_general | solution.py:13
  435.1 108.6 %while.16 = (s32[]{:T(128)}, f32[2,8,2,512]{3,2,1,0:T(2,128)}, s32[2,8]{1,0:T(2,128)S(1)}, s32[]{:T(128)}, f32[2,2048,512]{2,1,0:T(8,128)}, /*index=5*/s32[2,8,2...) while((s32[]{:T(128)}, f32[2,8,2,512]{3,2,1,0:T(2,128)}, ...), condition=%wide.region_6.7_spmd, body=%wide.region_4.6_spmd.sunk | while | flops 1649795328 | bytes 12208282 | solution.py:95
  435.6 8.9 %select_add_fusion.2 = f32[8,512,128]{2,1,0:T(8,128)S(1)} fusion(f32[8,512]{1,0:T(8,128)S(1)} %bitcast.278, s32[8,512]{1,0:T(8,128)S(1)} %get-tuple-element.357, f32[8,512]{1,0:T(8,128)S(1)} %bitcast.279, s32[8,512]{1,0:T(8,128)S(1)} %get-tuple-element.359, f32[8,512]{1,0:T(8,128)S(1)} %bitcast.280, s32[8,512]{1,0:T(8,128)S(1)} %get-tuple-element.361, ...), kind=kLoop, calls=%fused_computation.8.clone.1 | loop fusion | flops 12058624 | bytes 2359296 | tf_op jit(solution)/shard_map/while/body/eval_jaxpr/add | solution.py:67
  446.9 24.3 %while.17 = (s32[]{:T(128)}, f32[2,2048,512]{2,1,0:T(8,128)}, s32[8,3]{0,1:T(4,128)S(1)}, f32[8,2,128,128]{3,2,1,0:T(8,128)S(1)}, s32[]{:T(128)}) while((s32[]{:T(128)}, f32[2,2048,512]{2,1,0:T(8,128)}, s32[8,3]{0,1:T(4,128)S(1)}, f32[8,2,128,128]{3,2,1,0:T(8,128)S(1)}, s32[]{:T(128)}) %tuple.110), condition=%wide.while_cond, body=%wide.while_body.sunk | while | flops 2 | bytes 262261 | solution.py:152
  471.3 17.5 %fusion.256 = f32[8,2,512]{2,1,0:T(2,128)S(1)} fusion(f32[8,2,128,128]{3,2,1,0:T(8,128)S(1)} %get-tuple-element.351, f32[8,512,128]{1,2,0:T(8,128)} %copy.213, f32[8,512]{1,0:T(8,128)S(1)} %bitcast.287, s32[8,512]{1,0:T(8,128)S(1)} %get-tuple-element.374, f32[8,512]{1,0:T(8,128)S(1)} %bitcast.288, s32[8,512]{1,0:T(8,128)S(1)} %get-tuple-element.376, ...), kind=kOutput, calls=%fused_computation.6.clone.2 | convolution fusion | flops 1624760320 | bytes 3440640 | tf_op jit(solution)/shard_map/while/body/eval_jaxpr/gsu,gcuv->gcsv/dot_general | solution.py:13
  489.9 8.9 %select_add_fusion.2 = f32[8,512,128]{2,1,0:T(8,128)S(1)} fusion(f32[8,512]{1,0:T(8,128)S(1)} %bitcast.278, s32[8,512]{1,0:T(8,128)S(1)} %get-tuple-element.357, f32[8,512]{1,0:T(8,128)S(1)} %bitcast.279, s32[8,512]{1,0:T(8,128)S(1)} %get-tuple-element.359, f32[8,512]{1,0:T(8,128)S(1)} %bitcast.280, s32[8,512]{1,0:T(8,128)S(1)} %get-tuple-element.361, ...), kind=kLoop, calls=%fused_computation.8.clone.1 | loop fusion | flops 12058624 | bytes 2359296 | tf_op jit(solution)/shard_map/while/body/eval_jaxpr/add | solution.py:67
  501.2 24.4 %while.17 = (s32[]{:T(128)}, f32[2,2048,512]{2,1,0:T(8,128)}, s32[8,3]{0,1:T(4,128)S(1)}, f32[8,2,128,128]{3,2,1,0:T(8,128)S(1)}, s32[]{:T(128)}) while((s32[]{:T(128)}, f32[2,2048,512]{2,1,0:T(8,128)}, s32[8,3]{0,1:T(4,128)S(1)}, f32[8,2,128,128]{3,2,1,0:T(8,128)S(1)}, s32[]{:T(128)}) %tuple.110), condition=%wide.while_cond, body=%wide.while_body.sunk | while | flops 2 | bytes 262261 | solution.py:152
  525.6 17.5 %fusion.256 = f32[8,2,512]{2,1,0:T(2,128)S(1)} fusion(f32[8,2,128,128]{3,2,1,0:T(8,128)S(1)} %get-tuple-element.351, f32[8,512,128]{1,2,0:T(8,128)} %copy.213, f32[8,512]{1,0:T(8,128)S(1)} %bitcast.287, s32[8,512]{1,0:T(8,128)S(1)} %get-tuple-element.374, f32[8,512]{1,0:T(8,128)S(1)} %bitcast.288, s32[8,512]{1,0:T(8,128)S(1)} %get-tuple-element.376, ...), kind=kOutput, calls=%fused_computation.6.clone.2 | convolution fusion | flops 1624760320 | bytes 3440640 | tf_op jit(solution)/shard_map/while/body/eval_jaxpr/gsu,gcuv->gcsv/dot_general | solution.py:13
  543.7 4.3 all-to-all-start.3
  548.0 5.0 all-to-all-done.3
  (156 shorter events, 87.0 us)
Async XLA Ops:
  3.7 151.6 %all-to-all-start = ((s32[8,1,2]{2,1,0:T(1,128)}), s32[8,1,2]{2,1,0:T(1,128)S(1)}, u32[]{:S(2)}, u32[]{:S(2)}) async-start(s32[8,1,2]{2,1,0:T(1,128)} %bitcast.12), calls=%async_computation | async-start | bytes 8192 | tf_op jit(solution)/shard_map/all_to_all | solution.py:164
  17.3 26.1 %copy-start.3 = (f32[1,2048,512]{2,1,0:T(8,128)S(1)}, f32[1,2048,512]{2,1,0:T(8,128)}, u32[]{:S(2)}) copy-start(f32[1,2048,512]{2,1,0:T(8,128)} %get-tuple-element.232) | copy-start | bytes 12582916
  17.3 26.1 %copy-start.4 = (f32[1,2048,512]{2,1,0:T(8,128)S(1)}, f32[1,2048,512]{2,1,0:T(8,128)}, u32[]{:S(2)}) copy-start(f32[1,2048,512]{2,1,0:T(8,128)} %get-tuple-element.233) | copy-start | bytes 12582916
  155.3 6.4 %copy-start.6 = (s32[16,2,512]{2,1,0:T(2,128)S(1)}, s32[16,2,512]{2,1,0:T(2,128)}, u32[]{:S(2)}) copy-start(s32[16,2,512]{2,1,0:T(2,128)} %param.14) | copy-start | bytes 196612
  155.3 189.8 %all-to-all-start.1 = ((f32[4,2,512,512]{2,3,1,0:T(8,128)}), f32[4,2,512,512]{2,3,1,0:T(8,128)}, u32[]{:S(2)}, u32[]{:S(2)}) async-start(f32[4,2,512,512]{2,3,1,0:T(8,128)} %pad_maximum_fusion), calls=%async_computation.1 | async-start | bytes 16777216 | tf_op jit(solution)/shard_map/all_to_all | solution.py:121
  345.1 90.0 %all-to-all-start.2 = ((s32[8,2,2,512]{3,2,1,0:T(2,128)}), s32[8,2,2,512]{3,2,1,0:T(2,128)S(1)}, u32[]{:S(2)}, u32[]{:S(2)}) async-start(s32[8,2,2,512]{3,2,1,0:T(2,128)} %bitcast.33), calls=%async_computation.2 | async-start | bytes 131072 | tf_op jit(solution)/shard_map/all_to_all | solution.py:165
  362.1 10.2 %copy-start.1 = (f32[1,4,512,512]{3,2,1,0:T(8,128)S(1)}, f32[1,4,512,512]{3,2,1,0:T(8,128)}, u32[]{:S(2)}) copy-start(f32[1,4,512,512]{3,2,1,0:T(8,128)} %copy.62) | copy-start | bytes 12582916
  385.0 9.9 %copy-start = (f32[1,4,512,512]{3,2,1,0:T(8,128)S(1)}, f32[1,4,512,512]{3,2,1,0:T(8,128)}, u32[]{:S(2)}) copy-start(f32[1,4,512,512]{3,2,1,0:T(8,128)} %copy.60) | copy-start | bytes 12582916
  385.0 9.9 %copy-start.2 = (f32[128,16,512]{2,0,1:T(8,128)S(1)}, f32[128,16,512]{2,0,1:T(8,128)}, u32[]{:S(2)}) copy-start(f32[128,16,512]{2,0,1:T(8,128)} %fusion.62) | copy-start | bytes 12582916
  430.9 4.2 copy-start.5
  435.1 118.6 %copy-start.7 = (f32[16,2,512]{2,1,0:T(2,128)S(1)}, f32[16,2,512]{2,1,0:T(2,128)}, u32[]{:S(2)}) copy-start(f32[16,2,512]{2,1,0:T(2,128)} %param.15) | copy-start | bytes 196612
  543.7 9.3 %all-to-all-start.3 = ((f32[8,2,2,512]{3,2,1,0:T(2,128)}), f32[8,2,2,512]{3,2,1,0:T(2,128)S(1)}, u32[]{:S(2)}, u32[]{:S(2)}) async-start(f32[8,2,2,512]{3,2,1,0:T(2,128)} %bitcast.35), calls=%async_computation.3 | async-start | bytes 131072 | tf_op jit(solution)/shard_map/all_to_all | solution.py:175
